TPU v7x, 256 devices: a whole 4x4x8 slice. The times are simulated.
256 devices in a mesh: batch: 128 (over z, y, x_lo, core), rep: 2 (over x_hi).
Axes of the slice: x: 4 (x_hi: 2, x_lo: 2; x = x_hi * 2 + x_lo), y: 4, z: 8, core: 2. Of those that a mesh axis runs over, the one named last changes fastest.
Arguments:
- queries: bfloat16 [16384, 512], P('batch', 'rep'), may hold values from -8 to 8
- passages: bfloat16 [16384, 512], P('batch', 'rep'), may hold values from -8 to 8
- positives: int32 [16384], replicated, may hold values from 0 to 16383, each once
Outputs:
- grad_queries: float32 [16384, 512], P('batch', 'rep')
- grad_passages: float32 [16384, 512], P('batch', 'rep')
Inputs may be any that keep to these rules, and one draw needn't show every extreme that they name: `positives`: each passage is the positive of exactly one query.
All inputs are finite; a program needn't handle non-finite values.
Results may differ from a plain program's by a relative error of at most 0.0013.
Values may be sent and summed in bfloat16 or wider, within the bound.
A program may use at most 128 MiB of HBM per device.

v0:
```python
import math
import jax
import jax.numpy as jnp
from jax import lax
from jax.sharding import Mesh
from jax.sharding import PartitionSpec as P

BATCH = ("batch_0", "batch_1", "batch_2", "batch_3")
NEGATIVE = -1e30


def sent_together(arrays, axis, dim, along):
    both = jnp.concatenate(arrays, axis=along)
    filled, at, outs = (lax.all_gather(both, axis, axis=dim, tiled=True), 0, [])
    for a in arrays:
        outs.append(lax.slice_in_dim(filled, at, at + a.shape[along], axis=along))
        at += a.shape[along]
    return tuple(outs)


def copy_for_each(x, axis):
    count = lax.axis_size(axis)
    return lax.all_to_all(jnp.broadcast_to(x[None], (count, *x.shape)), axis, 0, 0, tiled=True)


def gathered_once(x, axis):
    leaves = jax.tree.leaves(x)
    order = sorted(range(len(leaves)), key=lambda k: -leaves[k].size)
    width = (1, *leaves[order[0]].shape)[-1]
    lines = [
        jnp.pad(leaves[k].reshape(-1), (0, -leaves[k].size % width)).reshape(-1, width)
        for k in order
    ]
    both, at, found = (copy_for_each(jnp.concatenate(lines), axis), 0, {})
    for k, line in zip(order, lines):
        section = both[:, at : at + len(line)].reshape(len(both), -1)
        found[k] = section[:, : leaves[k].size].reshape(-1, *leaves[k].shape)
        at += len(line)
    numbers = iter(range(len(leaves)))
    return jax.tree.map(lambda _: found[next(numbers)], x)


def combined_pairwise(pieces, combine):
    while len(jax.tree.leaves(pieces)[0]) > 1:
        pieces = jax.vmap(combine)(
            *(jax.tree.map(lambda part: part[side::2], pieces) for side in (0, 1))
        )
    return jax.tree.map(lambda part: part[0], pieces)


def joined_all(x, axis, combine):
    pieces = gathered_once(x, axis)
    return combined_pairwise(pieces, combine)


def collected_together(x, axis):
    leaves = jax.tree.leaves(x)
    order = sorted(range(len(leaves)), key=lambda k: -leaves[k].size)
    width = (1, *leaves[order[0]].shape)[-1]
    lines = [
        jnp.pad(leaves[k].reshape(-1), (0, -leaves[k].size % width)).reshape(-1, width)
        for k in order
    ]
    both, at, found = (lax.all_gather(jnp.concatenate(lines), axis), 0, {})
    for k, line in zip(order, lines):
        section = both[:, at : at + len(line)].reshape(len(both), -1)
        found[k] = section[:, : leaves[k].size].reshape(-1, *leaves[k].shape)
        at += len(line)
    numbers = iter(range(len(leaves)))
    return jax.tree.map(lambda _: found[next(numbers)], x)


def merged_by_axis(x, axes, combine):
    for axis in axes:
        pieces = collected_together(x, axis)
        x = jax.tree.map(lambda part: part[0], pieces)
        for k in range(1, lax.axis_size(axis)):
            x = combine(x, jax.tree.map(lambda part: part[k], pieces))
    return x


def joined_along(pieces, dim):
    pieces = jnp.moveaxis(pieces, 0, dim)
    dims = pieces.shape
    return pieces.reshape(*dims[:dim], dims[dim] * dims[dim + 1], *dims[dim + 2 :])


def stacked_from(x, axes, order):
    pieces = x
    for k in order:
        pieces = lax.all_gather(pieces, axes[k])
    done = order[::-1]
    back = [done.index(k) for k in range(len(axes))]
    pieces = pieces.transpose(*back, *range(len(axes), pieces.ndim))
    return pieces.reshape(-1, *x.shape)


def whole_of(x, axes, order, dim):
    return joined_along(stacked_from(x, axes, order), dim)


def collect(x, axis, dim):
    pieces = copy_for_each(x, axis)
    return joined_along(pieces, dim)


def in_blocks(x, dim, count):
    dims = x.shape
    pieces = x.reshape(*dims[:dim], count, dims[dim] // count, *dims[dim + 1 :])
    return jnp.moveaxis(pieces, dim, 0)


def summed_on_arrival(x, axis, dim):
    count = lax.axis_size(axis)
    pieces = lax.all_to_all(in_blocks(x, dim, count), axis, 0, 0, tiled=True)
    return jnp.sum(pieces, axis=0)


def sent_together_2(arrays, axis, dim, along):
    both = jnp.concatenate(arrays, axis=along)
    filled, at, outs = (summed_on_arrival(both, axis, dim), 0, [])
    for a in arrays:
        outs.append(lax.slice_in_dim(filled, at, at + a.shape[along], axis=along))
        at += a.shape[along]
    return tuple(outs)


def sweep_blocks(update, running, members):
    piece_rows = members[0].shape[0]

    def advance(carried, block_index):
        sliced = tuple(
            (lax.dynamic_slice_in_dim(member, block_index * 512, 512, 0) for member in members)
        )
        return (update(carried, sliced, block_index * 512), None)

    running, unused = lax.scan(advance, running, jnp.arange(piece_rows // 512, dtype=jnp.int32))
    return running


def combine_pairs(former, latter):
    results = []
    for position in range(0, len(former), 2):
        highest = jnp.maximum(former[position], latter[position])
        summed = former[position + 1] * jnp.exp(former[position] - highest) + latter[
            position + 1
        ] * jnp.exp(latter[position] - highest)
        results.extend([highest, summed])
    return tuple(results)


def pair_scores(local_set, remote_set, logit_scale):
    products = lax.dot_general(
        local_set, remote_set, (((1,), (1,)), ((), ())), preferred_element_type=jnp.float32
    )
    return products * logit_scale


def weighted_sum(
    local_set, local_norm, local_keys, remote_set, remote_norm, remote_keys, logit_scale
):
    scores = pair_scores(local_set, remote_set, logit_scale)
    matches = (local_keys[:, None] == remote_keys[None, :]).astype(jnp.float32)
    weights = (
        jnp.exp(scores - local_norm[:, None])
        + jnp.exp(scores - remote_norm[None, :])
        - 2.0 * matches
    )
    return jnp.dot(weights.astype(jnp.bfloat16), remote_set, preferred_element_type=jnp.float32)


def local(queries, passages, positives):
    own_rows = queries.shape[0]
    half_rows = own_rows // 2
    model_width = queries.shape[1] * lax.axis_size("rep")
    batch_count = lax.axis_size(BATCH)
    all_rows = batch_count * own_rows
    column_count = batch_count * half_rows
    logit_scale = 1.0 / math.sqrt(model_width)
    batch_index = lax.axis_index(BATCH)
    rep_index = lax.axis_index("rep")
    block_start = batch_index * own_rows
    half_start = rep_index * half_rows
    query_full, passage_full = sent_together((queries, passages), "rep", 1, 0)
    passage_half = lax.dynamic_slice_in_dim(passage_full, half_start, half_rows, 0)

    def score_update(running, sliced, offset):
        row_high, row_total, column_high, column_total = running
        scores = pair_scores(query_full, sliced[0], logit_scale)
        new_high = jnp.maximum(row_high, jnp.max(scores, axis=1))
        row_total = row_total * jnp.exp(row_high - new_high) + jnp.sum(
            jnp.exp(scores - new_high[:, None]), axis=1
        )
        piece_high = jnp.max(scores, axis=0)
        piece_total = jnp.sum(jnp.exp(scores - piece_high[None, :]), axis=0)
        column_high = lax.dynamic_update_slice_in_dim(column_high, piece_high, offset, 0)
        column_total = lax.dynamic_update_slice_in_dim(column_total, piece_total, offset, 0)
        return (new_high, row_total, column_high, column_total)

    starting = (
        jnp.full((own_rows,), NEGATIVE, jnp.float32),
        jnp.zeros((own_rows,), jnp.float32),
        jnp.full((column_count,), NEGATIVE, jnp.float32),
        jnp.zeros((column_count,), jnp.float32),
    )
    row_high, row_total, column_high, column_total = sweep_blocks(
        score_update, starting, (lax.all_gather(passage_half, BATCH, axis=0, tiled=True),)
    )
    row_high, row_total = joined_all((row_high, row_total), "rep", combine_pairs)
    column_high, column_total = merged_by_axis((column_high, column_total), BATCH, combine_pairs)
    row_norms = whole_of(row_high + jnp.log(row_total), BATCH, (2, 0, 1, 3), 0)
    column_halves = collect(column_high + jnp.log(column_total), "rep", 0)
    column_norms = (
        column_halves.reshape(2, batch_count, half_rows).transpose(1, 0, 2).reshape(all_rows)
    )
    row_own = lax.dynamic_slice_in_dim(row_norms, block_start, own_rows, 0)
    column_own = lax.dynamic_slice_in_dim(column_norms, block_start, own_rows, 0)
    positive_own = lax.dynamic_slice_in_dim(positives, block_start, own_rows, 0)
    own_ids = block_start + jnp.arange(own_rows, dtype=jnp.int32)
    all_ids = jnp.arange(all_rows, dtype=jnp.int32)
    cleared = jnp.zeros((own_rows, model_width), jnp.float32)

    def half_order(vector):
        return lax.dynamic_slice_in_dim(
            vector.reshape(batch_count, own_rows), half_start, half_rows, 1
        ).reshape(column_count)

    column_order = half_order(column_norms)
    row_order = half_order(row_norms)
    positive_order = half_order(positives)
    passage_order = half_order(all_ids)
    query_half = lax.dynamic_slice_in_dim(query_full, half_start, half_rows, 0)

    def both_update(running, sliced, offset):
        query_sum, passage_sum = running
        passage_piece, query_piece = sliced
        piece_rows = passage_piece.shape[0]

        def window(vector):
            return lax.dynamic_slice_in_dim(vector, offset, piece_rows, 0)

        query_sum = query_sum + weighted_sum(
            query_full,
            row_own,
            positive_own,
            passage_piece,
            window(column_order),
            window(passage_order),
            logit_scale,
        )
        passage_sum = passage_sum + weighted_sum(
            passage_full,
            column_own,
            own_ids,
            query_piece,
            window(row_order),
            window(positive_order),
            logit_scale,
        )
        return (query_sum, passage_sum)

    query_sum, passage_sum = sweep_blocks(
        both_update, (cleared, cleared), sent_together((passage_half, query_half), BATCH, 0, 1)
    )
    grad_queries, grad_passages = sent_together_2(
        (query_sum * logit_scale, passage_sum * logit_scale), "rep", 1, 0
    )
    return (grad_queries, grad_passages)


def solution(mesh):
    split = Mesh(
        mesh.devices.reshape(8, 4, 2, 2, mesh.shape["rep"]),
        ("batch_0", "batch_1", "batch_2", "batch_3", "rep"),
    )
    return jax.shard_map(
        local,
        mesh=split,
        in_specs=(P(BATCH, "rep"), P(BATCH, "rep"), P()),
        out_specs=(P(BATCH, "rep"), P(BATCH, "rep")),
        check_vma=False,
    )
```

profile of v0, /device:TPU:32, one launch (start us, length us, event | category | flops | bytes accessed | tf_op | source)
XLA Modules:
  0.0 585.7 jit_solution(4580716487339270084)
XLA Ops:
  8.1 7.4 %all_gather.55 = bf16[256,512]{1,0:T(8,128)(2,1)S(1)} all-gather(bf16[256,256]{1,0:T(8,128)(2,1)S(1)} %pad_maximum_fusion.1), channel_id=1, replica_groups=mesh['batch_0'=8,'batch_1'=4,'batch_2'=2,'batch_3'=2,'rep'=2] {'rep'}, dimensions={1}, use_global_device_ids=true | all-gather | bytes 393216 | tf_op jit(solution)/shard_map/all_gather | solution.py:14
  19.7 219.5 %all-gather.18.cloned.1.call-done = bf16[8192,512]{1,0:T(8,128)(2,1)} async-done(((bf16[64,512]{1,0:T(8,128)(2,1)}), bf16[8192,512]{1,0:T(8,128)(2,1)}) %all-gather.18.cloned.1.call-update) | async-done | bytes 8388624 | tf_op jit(solution)/shard_map/all_gather | solution.py:207
  239.2 55.7 %while.30 = (s32[]{:T(128)}, f32[128]{0:T(128)S(1)}, f32[128]{0:T(128)S(1)}, f32[8192]{0:T(1024)S(1)}, f32[8192]{0:T(1024)S(1)}, /*index=5*/s32[16]{0:T(128)S(1)...) while((s32[]{:T(128)}, f32[128]{0:T(128)S(1)}, ...), condition=%wide.region_5.6_spmd.clone, body=%wide.region_0.5_spmd.clone.sunk | while | flops 67567240 | bytes 1200838 | solution.py:137
  295.5 4.3 all-to-all-start
  299.9 25.0 %all-gather.9 = f32[8,2,8192]{2,1,0:T(2,128)S(1)} all-gather(f32[1,2,8192]{2,1,0:T(2,128)S(1)} %maximum_bitcast_fusion), channel_id=5, replica_groups=mesh['batch_0'=8,'batch_1'=4,'batch_2'=2,'batch_3'=2,'rep'=2] {'batch_0'}, dimensions={0}, use_global_device_ids=true | all-gather | bytes 589824 | tf_op jit(solution)/shard_map/all_gather | solution.py:64
  325.8 12.3 %all-gather.10 = f32[4,2,8192]{2,1,0:T(2,128)S(1)} all-gather(f32[1,2,8192]{2,1,0:T(2,128)S(1)} %maximum_bitcast_fusion.1), channel_id=6, replica_groups=mesh['batch_0'=8,'batch_1'=4,'batch_2'=2,'batch_3'=2,'rep'=2] {'batch_1'}, dimensions={0}, use_global_device_ids=true | all-gather | bytes 327680 | tf_op jit(solution)/shard_map/all_gather | solution.py:64
  338.4 4.9 all-gather.11
  343.5 1.9 all-gather.12
  346.3 5.0 all-to-all-start.1
  351.3 4.2 all-gather.7
  355.5 14.3 %all-gather.8 = f32[8,2,128]{2,1,0:T(2,128)S(1)} all-gather(f32[1,2,128]{2,1,0:T(2,128)S(1)} %bitcast.357), channel_id=2, replica_groups=mesh['batch_0'=8,'batch_1'=4,'batch_2'=2,'batch_3'=2,'rep'=2] {'batch_0'}, dimensions={0}, use_global_device_ids=true | all-gather | bytes 9216 | tf_op jit(solution)/shard_map/all_gather | solution.py:91
  369.8 11.9 %all-gather.1 = f32[32,2,128]{2,1,0:T(2,128)S(1)} all-gather(f32[8,2,128]{2,1,0:T(2,128)S(1)} %all-gather.8), channel_id=3, replica_groups=mesh['batch_0'=8,'batch_1'=4,'batch_2'=2,'batch_3'=2,'rep'=2] {'batch_1'}, dimensions={0}, use_global_device_ids=true | all-gather | bytes 40960 | tf_op jit(solution)/shard_map/all_gather | solution.py:91
  384.8 83.6 %all-gather.16.cloned.1.call-done = bf16[8192,1024]{1,0:T(8,128)(2,1)} async-done(((bf16[64,1024]{1,0:T(8,128)(2,1)}), bf16[8192,1024]{1,0:T(8,128)(2,1)}) %all-gather.16.cloned.1.call-update) | async-done | bytes 16777232 | tf_op jit(solution)/shard_map/all_gather | solution.py:14
  468.4 11.3 %fusion.101 = (bf16[8192,512]{1,0:T(8,128)(2,1)}, bf16[8192,512]{1,0:T(8,128)(2,1)}) fusion(bf16[8192,1024]{1,0:T(8,128)(2,1)} %all-gather.16.cloned.1.call-done), kind=kLoop, calls=%fused_computation.152 | loop fusion | bytes 33554432 | tf_op jit(solution)/shard_map/slice | solution.py:16
  479.7 86.1 %while.31 = (s32[]{:T(128)}, f32[128,512]{1,0:T(8,128)S(1)}, f32[128,512]{1,0:T(8,128)S(1)}, s32[16]{0:T(128)S(1)}, bf16[8192,512]{1,0:T(8,128)(2,1)}, /*index=5...) while((s32[]{:T(128)}, f32[128,512]{1,0:T(8,128)S(1)}, ...), condition=%wide.region_7.8_spmd.clone, body=%wide.region_6.7_spmd.clone.sunk | while | flops 269746304 | bytes 3438348 | solution.py:137
  481.1 2.0 convolution_add_fusion.5
  483.3 1.9 convolution_add_fusion.4
  486.6 1.9 convolution_add_fusion.5
  488.6 1.9 convolution_add_fusion.4
  502.7 1.9 convolution_add_fusion.5
  504.7 1.9 convolution_add_fusion.4
  508.1 1.9 convolution_add_fusion.5
  513.5 1.9 convolution_add_fusion.5
  526.2 1.9 convolution_add_fusion.4
  529.5 1.9 convolution_add_fusion.5
  531.6 1.9 convolution_add_fusion.4
  540.3 1.9 convolution_add_fusion.5
  547.7 1.9 convolution_add_fusion.4
  551.1 1.9 convolution_add_fusion.5
  558.5 1.9 convolution_add_fusion.4
  563.8 1.9 convolution_add_fusion.4
  566.4 11.7 %all_to_all.16 = f32[2,256,256]{2,1,0:T(8,128)S(1)} all-to-all(f32[2,256,256]{2,1,0:T(8,128)S(1)} %copy.28), channel_id=1, replica_groups=mesh['batch_0'=8,'batch_1'=4,'batch_2'=2,'batch_3'=2,'rep'=2] {'rep'}, dimensions={0} | all-to-all | bytes 1048576 | tf_op jit(solution)/shard_map/all_to_all | solution.py:115
  (299 shorter events, 101.4 us)
Async XLA Ops:
  7.2 232.0 %all-gather.18.cloned.1.call-start = ((), (), s32[]{:S(2)}) async-start(), calls=%async_computation.4 | async-start | bytes 8454144 | tf_op jit(solution)/shard_map/all_gather | solution.py:207
  16.2 452.2 %all-gather.16.cloned.1.call-start = ((), (), s32[]{:S(2)}) async-start(), calls=%async_computation.3 | async-start | bytes 16908288 | tf_op jit(solution)/shard_map/all_gather | solution.py:14
  295.5 50.1 %all-to-all-start = ((f32[2,2,128]{2,1,0:T(2,128)}), f32[2,2,128]{2,1,0:T(2,128)S(1)}, u32[]{:S(2)}, u32[]{:S(2)}) async-start(f32[2,2,128]{2,1,0:T(2,128)} %broadcast_in_dim.21), calls=%async_computation | async-start | bytes 4096 | tf_op jit(solution)/shard_map/all_to_all | solution.py:23
  346.3 37.6 %all-to-all-start.1 = ((f32[2,1,8192]{2,1,0:T(1,128)}), f32[2,1,8192]{2,1,0:T(1,128)S(1)}, u32[]{:S(2)}, u32[]{:S(2)}) async-start(f32[2,1,8192]{2,1,0:T(1,128)} %broadcast_in_dim.22), calls=%async_computation.1 | async-start | bytes 131072 | tf_op jit(solution)/shard_map/all_to_all | solution.py:23
Sparse Core Ops, SparseCore 0:
  16.3 222.8 all-gather.17
  241.6 226.7 all-gather.15
where the time goes:
time: 588 us; the launch traced here: 586 us
  waiting for transfers between devices  303 us (52%)
  blocking collectives  95.6 us (16%)
  matrix products  83.6 us (14%)
  local copies, waits for them, and re-layouts  48.4 us (8%)
  loops' own time  22 us (4%)
  between operations  14.3 us (2%)
  starting transfers between devices  9.39 us (2%)
  other arithmetic  9.37 us (2%)
    all_gather x1, waiting for transfers between devices, local(): lax.all_gather(passage_half, BATCH, axis=0, tiled=True)  220 us
    all_gather x1, waiting for transfers between devices, sent_together(): filled, at, outs = (lax.all_gather(both, axis, axis=dim, tiled=True), 0, [])  83.6 us
    dot_general x32, matrix products, weighted_sum(): jnp.dot(weights.astype(jnp.bfloat16), remote_set, preferred_element_type=...  60.7 us
    all_gather x4, blocking collectives, collected_together(): both, at, found = (lax.all_gather(jnp.concatenate(lines), axis), 0, {})  44.1 us
    all_gather x4, blocking collectives, stacked_from(): pieces = lax.all_gather(pieces, axes[k])  32.3 us
    dot_general x16, matrix products, pair_scores(): lax.dot_general(local_set, remote_set, (((1,), (1,)), ((), ())), preferre...  22.8 us
    another operation x2, loops' own time, sweep_blocks(): lax.scan(advance, running, jnp.arange(piece_rows // 512, dtype=jnp.int32))  22 us
    dynamic_slice x32, local copies, waits for them, and re-layouts, sweep_blocks(): lax.scan(advance, running, jnp.arange(piece_rows // 512, dtype=jnp.int32))  18.8 us
  transfers between devices with their start and end apart: 4, of which 2 were waited for; matrix products, arithmetic and copies ran while one was open for 9% of the time, Pallas kernels for 0%

commit v1 on v0

--- a/solution.py
+++ b/solution.py
@@ -204,7 +204,14 @@
         jnp.zeros((column_count,), jnp.float32),
     )
     row_high, row_total, column_high, column_total = sweep_blocks(
-        score_update, starting, (lax.all_gather(passage_half, BATCH, axis=0, tiled=True),)
+        score_update,
+        starting,
+        (
+            jnp.concatenate(
+                lax.all_to_all(jnp.stack([passage_half] * lax.axis_size(BATCH)), BATCH, 0, 0),
+                axis=0,
+            ),
+        ),
     )
     row_high, row_total = joined_all((row_high, row_total), "rep", combine_pairs)
     column_high, column_total = merged_by_axis((column_high, column_total), BATCH, combine_pairs)

time: 588 us -> 535 us (0.910)
  waiting for transfers between devices: 303 us -> 234 us
  starting transfers between devices: 9.39 us -> 22.8 us
    all_to_all x0 -> x1, waiting for transfers between devices: none -> 234 us  [local(): lax.all_to_all(jnp.stack([passage_half] * lax.axis_size(BATCH)), BATCH, 0...]
    all_gather x1 -> x0, waiting for transfers between devices: 220 us -> none  [local(): lax.all_gather(passage_half, BATCH, axis=0, tiled=True)]
    all_gather x1, waiting for transfers between devices: 83.6 us -> 0.01 us  [sent_together(): filled, at, outs = (lax.all_gather(both, axis, axis=dim, tiled=True), 0, [])]
    all_to_all x0 -> x1, starting transfers between devices: none -> 14.1 us  [local(): lax.all_to_all(jnp.stack([passage_half] * lax.axis_size(BATCH)), BATCH, 0...]
  transfers between devices with their start and end apart: 4 -> 4, of which waited for: 2 -> 1; matrix products, arithmetic and copies ran while one was open for 9% -> 9% of each run, Pallas kernels for 0% -> 0%
where the time goes in v1:
time: 535 us; the launch traced here: 531 us
  waiting for transfers between devices  234 us (44%)
  blocking collectives  97.7 us (18%)
  matrix products  83.5 us (16%)
  local copies, waits for them, and re-layouts  50.9 us (10%)
  starting transfers between devices  22.8 us (4%)
  loops' own time  20.4 us (4%)
  between operations  14.3 us (3%)
  other arithmetic  7.69 us (1%)
    all_to_all x1, waiting for transfers between devices, local(): lax.all_to_all(jnp.stack([passage_half] * lax.axis_size(BATCH)), BATCH, 0...  234 us
    dot_general x32, matrix products, weighted_sum(): jnp.dot(weights.astype(jnp.bfloat16), remote_set, preferred_element_type=...  60.7 us
    all_gather x4, blocking collectives, collected_together(): both, at, found = (lax.all_gather(jnp.concatenate(lines), axis), 0, {})  43.3 us
    all_gather x4, blocking collectives, stacked_from(): pieces = lax.all_gather(pieces, axes[k])  32.6 us
    dot_general x16, matrix products, pair_scores(): lax.dot_general(local_set, remote_set, (((1,), (1,)), ((), ())), preferre...  22.8 us
    another operation x2, loops' own time, sweep_blocks(): lax.scan(advance, running, jnp.arange(piece_rows // 512, dtype=jnp.int32))  20.4 us
    dynamic_slice x32, local copies, waits for them, and re-layouts, sweep_blocks(): lax.scan(advance, running, jnp.arange(piece_rows // 512, dtype=jnp.int32))  18.3 us
    all_to_all x1, blocking collectives, summed_on_arrival(): pieces = lax.all_to_all(in_blocks(x, dim, count), axis, 0, 0, tiled=True)  14.4 us
  transfers between devices with their start and end apart: 4, of which 1 were waited for; matrix products, arithmetic and copies ran while one was open for 9% of the time, Pallas kernels for 0%

profile of v1, /device:TPU:32, one launch (start us, length us, event | category | flops | bytes accessed | tf_op | source)
XLA Modules:
  0.0 531.2 jit_solution(10713568677704161086)
XLA Ops:
  8.1 7.4 %all_gather.52 = bf16[256,512]{1,0:T(8,128)(2,1)S(1)} all-gather(bf16[256,256]{1,0:T(8,128)(2,1)S(1)} %pad_maximum_fusion.1), channel_id=1, replica_groups=mesh['batch_0'=8,'batch_1'=4,'batch_2'=2,'batch_3'=2,'rep'=2] {'rep'}, dimensions={1}, use_global_device_ids=true | all-gather | bytes 393216 | tf_op jit(solution)/shard_map/all_gather | solution.py:14
  15.5 4.3 stack.2
  19.8 14.1 %all-to-all-start = ((bf16[128,64,512]{2,1,0:T(8,128)(2,1)}), bf16[128,64,512]{2,1,0:T(8,128)(2,1)}, u32[]{:S(2)}, u32[]{:S(2)}) async-start(bf16[128,64,512]{2,1,0:T(8,128)(2,1)} %stack.2), calls=%async_computation | async-start | bytes 16777216 | tf_op jit(solution)/shard_map/all_to_all | solution.py:211
  35.0 234.1 %all-to-all-done = bf16[128,64,512]{2,1,0:T(8,128)(2,1)} async-done(((bf16[128,64,512]{2,1,0:T(8,128)(2,1)}), bf16[128,64,512]{2,1,0:T(8,128)(2,1)}, u32[]{:S(2)}, u32[]{:S(2)}) %all-to-all-start) | async-done | bytes 8388640 | tf_op jit(solution)/shard_map/all_to_all | solution.py:211
  269.0 53.6 %while.30 = (s32[]{:T(128)}, f32[128]{0:T(128)S(1)}, f32[128]{0:T(128)S(1)}, f32[8192]{0:T(1024)S(1)}, f32[8192]{0:T(1024)S(1)}, /*index=5*/s32[16]{0:T(128)S(1)...) while((s32[]{:T(128)}, f32[128]{0:T(128)S(1)}, ...), condition=%wide.region_5.6_spmd.clone, body=%wide.region_0.5_spmd.clone.sunk | while | flops 67567240 | bytes 1200838 | solution.py:137
  323.2 3.9 all-to-all-start.1
  327.2 24.2 %all-gather.9 = f32[8,2,8192]{2,1,0:T(2,128)S(1)} all-gather(f32[1,2,8192]{2,1,0:T(2,128)S(1)} %maximum_bitcast_fusion), channel_id=5, replica_groups=mesh['batch_0'=8,'batch_1'=4,'batch_2'=2,'batch_3'=2,'rep'=2] {'batch_0'}, dimensions={0}, use_global_device_ids=true | all-gather | bytes 589824 | tf_op jit(solution)/shard_map/all_gather | solution.py:64
  352.2 12.3 %all-gather.10 = f32[4,2,8192]{2,1,0:T(2,128)S(1)} all-gather(f32[1,2,8192]{2,1,0:T(2,128)S(1)} %maximum_bitcast_fusion.1), channel_id=6, replica_groups=mesh['batch_0'=8,'batch_1'=4,'batch_2'=2,'batch_3'=2,'rep'=2] {'batch_1'}, dimensions={0}, use_global_device_ids=true | all-gather | bytes 327680 | tf_op jit(solution)/shard_map/all_gather | solution.py:64
  364.9 4.9 all-gather.11
  370.0 1.9 all-gather.12
  372.8 4.7 all-to-all-start.2
  377.5 4.2 all-gather.7
  381.7 14.6 %all-gather.8 = f32[8,2,128]{2,1,0:T(2,128)S(1)} all-gather(f32[1,2,128]{2,1,0:T(2,128)S(1)} %bitcast.358), channel_id=2, replica_groups=mesh['batch_0'=8,'batch_1'=4,'batch_2'=2,'batch_3'=2,'rep'=2] {'batch_0'}, dimensions={0}, use_global_device_ids=true | all-gather | bytes 9216 | tf_op jit(solution)/shard_map/all_gather | solution.py:91
  396.3 11.9 %all-gather.1 = f32[32,2,128]{2,1,0:T(2,128)S(1)} all-gather(f32[8,2,128]{2,1,0:T(2,128)S(1)} %all-gather.8), channel_id=3, replica_groups=mesh['batch_0'=8,'batch_1'=4,'batch_2'=2,'batch_3'=2,'rep'=2] {'batch_1'}, dimensions={0}, use_global_device_ids=true | all-gather | bytes 40960 | tf_op jit(solution)/shard_map/all_gather | solution.py:91
  411.3 11.3 %fusion.101 = (bf16[8192,512]{1,0:T(8,128)(2,1)}, bf16[8192,512]{1,0:T(8,128)(2,1)}) fusion(bf16[8192,1024]{1,0:T(8,128)(2,1)} %all-gather.15.cloned.1.call-done), kind=kLoop, calls=%fused_computation.152 | loop fusion | bytes 33554432 | tf_op jit(solution)/shard_map/slice | solution.py:16
  422.6 86.1 %while.31 = (s32[]{:T(128)}, f32[128,512]{1,0:T(8,128)S(1)}, f32[128,512]{1,0:T(8,128)S(1)}, s32[16]{0:T(128)S(1)}, bf16[8192,512]{1,0:T(8,128)(2,1)}, /*index=5...) while((s32[]{:T(128)}, f32[128,512]{1,0:T(8,128)S(1)}, ...), condition=%wide.region_7.8_spmd.clone, body=%wide.region_6.7_spmd.clone.sunk | while | flops 269746304 | bytes 3438348 | solution.py:137
  424.0 2.0 convolution_add_fusion.5
  426.1 1.9 convolution_add_fusion.4
  431.5 1.9 convolution_add_fusion.4
  445.6 1.9 convolution_add_fusion.5
  447.6 1.9 convolution_add_fusion.4
  450.9 1.9 convolution_add_fusion.5
  456.3 1.9 convolution_add_fusion.5
  469.1 1.9 convolution_add_fusion.4
  472.4 1.9 convolution_add_fusion.5
  474.5 1.9 convolution_add_fusion.4
  483.2 1.9 convolution_add_fusion.5
  490.6 1.9 convolution_add_fusion.4
  493.9 1.9 convolution_add_fusion.5
  501.3 1.9 convolution_add_fusion.4
  506.7 1.9 convolution_add_fusion.4
  509.2 14.4 %all_to_all.21 = f32[2,256,256]{2,1,0:T(8,128)S(1)} all-to-all(f32[2,256,256]{2,1,0:T(8,128)S(1)} %copy.28), channel_id=1, replica_groups=mesh['batch_0'=8,'batch_1'=4,'batch_2'=2,'batch_3'=2,'rep'=2] {'rep'}, dimensions={0} | all-to-all | bytes 1048576 | tf_op jit(solution)/shard_map/all_to_all | solution.py:115
  (301 shorter events, 99.7 us)
Async XLA Ops:
  19.8 14.9 %copy-start = (s32[16384]{0:T(1024)S(1)}, s32[16384]{0:T(1024)}, u32[]{:S(2)}) copy-start(s32[16384]{0:T(1024)} %param.9) | copy-start | bytes 196612
  19.8 249.3 %all-to-all-start = ((bf16[128,64,512]{2,1,0:T(8,128)(2,1)}), bf16[128,64,512]{2,1,0:T(8,128)(2,1)}, u32[]{:S(2)}, u32[]{:S(2)}) async-start(bf16[128,64,512]{2,1,0:T(8,128)(2,1)} %stack.2), calls=%async_computation | async-start | bytes 16777216 | tf_op jit(solution)/shard_map/all_to_all | solution.py:211
  33.8 377.4 %all-gather.15.cloned.1.call-start = ((), (), s32[]{:S(2)}) async-start(), calls=%async_computation.4 | async-start | bytes 16908288 | tf_op jit(solution)/shard_map/all_gather | solution.py:14
  323.2 48.9 %all-to-all-start.1 = ((f32[2,2,128]{2,1,0:T(2,128)}), f32[2,2,128]{2,1,0:T(2,128)S(1)}, u32[]{:S(2)}, u32[]{:S(2)}) async-start(f32[2,2,128]{2,1,0:T(2,128)} %broadcast_in_dim.21), calls=%async_computation.1 | async-start | bytes 4096 | tf_op jit(solution)/shard_map/all_to_all | solution.py:23
  372.8 37.6 %all-to-all-start.2 = ((f32[2,1,8192]{2,1,0:T(1,128)}), f32[2,1,8192]{2,1,0:T(1,128)S(1)}, u32[]{:S(2)}, u32[]{:S(2)}) async-start(f32[2,1,8192]{2,1,0:T(1,128)} %broadcast_in_dim.22), calls=%async_computation.2 | async-start | bytes 131072 | tf_op jit(solution)/shard_map/all_to_all | solution.py:23
Sparse Core Ops, SparseCore 0:
  37.1 325.7 all-gather.14
